TPU v7x, 32 devices: a whole 2x2x4 slice. The times are simulated.
32 devices in a mesh: prow: 4 (over x, core), pcol: 8 (over z, y).
Axes of the slice: x: 2, y: 2, z: 4, core: 2. Of those that a mesh axis runs over, the one named last changes fastest.
Arguments:
- slab: float32 [16384, 2048], P('prow', 'pcol'), may hold values from -6 to 6
- panel: float32 [16384, 512], P(('prow', 'pcol')), may hold values from -0.25 to 0.25
- pivots: int32 [512], replicated, may hold values from 0 to 16383, as said below
- inv_lower: float32 [512, 512], replicated, as said below
- inv_upper: float32 [512, 512], replicated, as said below
Outputs:
- updated: float32 [16384, 2048], P('prow', 'pcol')
Inputs may be any that keep to these rules, and one draw needn't show every extreme that they name: `pivots`: 512 distinct row indices. `inv_lower`: unit lower triangular. `inv_upper`: upper triangular with a positive diagonal.
All inputs are finite; a program needn't handle non-finite values.
Results may differ from a plain program's by a relative error of at most 0.000061.
Values sent between devices are 32-bit elements; how exact they have to be, the bound alone decides.
A program may use at most 64 MiB of HBM per device.

v0:
```python
import jax
import jax.numpy as jnp
from jax import lax
from jax.sharding import PartitionSpec as P


def local(slab, panel, pivots, inv_lower, inv_upper):
    row_count = slab.shape[0]
    first_row = lax.axis_index("prow") * row_count
    local_index = pivots - first_row
    inside = (local_index >= 0) & (local_index < row_count)
    safe_index = jnp.where(inside, local_index, 0)
    picked = jnp.where(inside[:, None], jnp.take(slab, safe_index, axis=0), 0.0)
    pivot_rows = lax.psum(picked, "prow")
    upper_block = jnp.dot(
        inv_lower, pivot_rows, precision=lax.Precision.HIGHEST, preferred_element_type=jnp.float32
    )
    own_lower = jnp.dot(
        panel, inv_upper, precision=lax.Precision.HIGHEST, preferred_element_type=jnp.float32
    )
    product = jnp.dot(
        lax.all_gather(own_lower, "pcol", axis=0, tiled=True),
        upper_block,
        precision=lax.Precision.HIGHEST,
        preferred_element_type=jnp.float32,
    )
    updated = slab - product
    target = jnp.where(inside, local_index, row_count)
    return updated.at[target].set(upper_block, mode="drop")


def solution(mesh):
    return jax.shard_map(
        local,
        mesh=mesh,
        in_specs=(P("prow", "pcol"), P(("prow", "pcol"), None), P(), P(), P()),
        out_specs=P("prow", "pcol"),
        check_vma=False,
    )
```

profile of v0, /device:TPU:0, one launch (start us, length us, event | category | flops | bytes accessed | tf_op | source)
XLA Modules:
  0.0 168.0 jit_solution(13603019011698801581)
XLA Ops:
  7.4 0.0 copy-start
  7.4 0.0 copy-start.1
  7.4 0.0 all-reduce.2.cloned.1.call-start
  7.4 0.8 compare_and_fusion
  8.2 0.0 copy-start.3
  8.2 3.8 %gather_fusion = f32[512,256]{1,0:T(8,128)S(1)} fusion(f32[4096,256]{1,0:T(8,128)} %param.5, s32[1024]{0:T(1024)S(1)} %pad_clamp_fusion), kind=kCustom, calls=%fused_computation | custom fusion | bytes 1050624 | tf_op jit(solution)/shard_map/jit(_take)/gather | solution.py:13
  12.0 1.0 select_select_fusion
  13.0 0.0 copy-start.2
  13.0 0.0 all-reduce.2.cloned.1.call-update
  13.1 0.0 all-gather.2.cloned.1.call-start
  13.1 0.0 copy-done
  13.1 0.0 copy-done.1
  13.1 2.8 %fusion = f32[512,512]{1,0:T(8,128)} fusion(f32[512,512]{1,0:T(8,128)S(1)} %copy-done, f32[512,512]{1,0:T(8,128)S(1)} %copy-done.1), kind=kOutput, calls=%fused_computation.9 | convolution fusion | flops 1610612736 | bytes 3145728 | tf_op jit(solution)/shard_map/dot_general | solution.py:18
  16.0 0.0 all-gather.2.cloned.1.call-update
  16.0 0.0 copy-done.3
  16.0 33.5 %all-reduce.2.cloned.1.call-done = f32[512,256]{1,0:T(8,128)} async-done(((f32[512,256]{1,0:T(8,128)}), f32[512,256]{1,0:T(8,128)}) %all-reduce.2.cloned.1.call-update) | async-done | bytes 524304 | tf_op jit(solution)/shard_map/psum | solution.py:14
  49.5 0.0 copy-done.2
  49.5 2.9 %fusion.1 = f32[256,512]{1,0:T(8,128)S(1)} fusion(f32[512,256]{1,0:T(8,128)} %all-reduce.2.cloned.1.call-done, f32[512,512]{1,0:T(8,128)S(1)} %copy-done.2), kind=kOutput, calls=%fused_computation.10 | convolution fusion | flops 805306368 | bytes 2097152 | tf_op jit(solution)/shard_map/dot_general | solution.py:15
  52.4 0.2 copy.6
  52.6 90.4 %all-gather.2.cloned.1.call-done = f32[4096,512]{1,0:T(8,128)} async-done(((f32[512,512]{1,0:T(8,128)}), f32[4096,512]{1,0:T(8,128)}) %all-gather.2.cloned.1.call-update) | async-done | bytes 8388624 | tf_op jit(solution)/shard_map/all_gather | solution.py:22
  143.0 11.2 %convolution_subtract_fusion = f32[4096,256]{1,0:T(8,128)} fusion(f32[4096,256]{1,0:T(8,128)} %param.5, f32[4096,512]{1,0:T(8,128)} %all-gather.2.cloned.1.call-done, f32[256,512]{1,0:T(8,128)S(1)} %fusion.1), kind=kOutput, calls=%fused_computation.2 | convolution fusion | flops 6443499520 | bytes 17301504 | tf_op jit(solution)/shard_map/dot_general | solution.py:21
  154.2 6.4 %scatter_fusion = f32[4096,256]{1,0:T(8,128)} fusion(f32[4096,256]{1,0:T(8,128)} %convolution_subtract_fusion, s32[512]{0:T(512)S(1)} %compare_select_fusion, f32[512,256]{1,0:T(8,128)S(1)} %copy.6), kind=kCustom, calls=%fused_computation.1 | custom fusion | bytes 1574912 | tf_op jit(solution)/shard_map/scatter | solution.py:29
  (2 shorter events, 0.0 us)
Async XLA Ops:
  7.4 5.8 %copy-start = (f32[512,512]{1,0:T(8,128)S(1)}, f32[512,512]{1,0:T(8,128)}, u32[]{:S(2)}) copy-start(f32[512,512]{1,0:T(8,128)} %param.6) | copy-start | bytes 3145732
  7.4 5.8 %copy-start.1 = (f32[512,512]{1,0:T(8,128)S(1)}, f32[512,512]{1,0:T(8,128)}, u32[]{:S(2)}) copy-start(f32[512,512]{1,0:T(8,128)} %param.9) | copy-start | bytes 3145732
  7.4 42.1 %all-reduce.2.cloned.1.call-start = ((), (), s32[]{:S(2)}) async-start(), calls=%async_computation.1 | async-start | bytes 1048576 | tf_op jit(solution)/shard_map/psum | solution.py:14
  8.2 7.8 %copy-start.3 = (s32[512]{0:T(512)S(1)}, s32[512]{0:T(512)}, u32[]{:S(2)}) copy-start(s32[512]{0:T(512)} %param.7) | copy-start | bytes 6148
  13.0 36.4 %copy-start.2 = (f32[512,512]{1,0:T(8,128)S(1)}, f32[512,512]{1,0:T(8,128)}, u32[]{:S(2)}) copy-start(f32[512,512]{1,0:T(8,128)} %param.8) | copy-start | bytes 3145732
  13.1 129.9 %all-gather.2.cloned.1.call-start = ((), (), s32[]{:S(2)}) async-start(), calls=%async_computation | async-start | bytes 9437184 | tf_op jit(solution)/shard_map/all_gather | solution.py:22
Sparse Core Ops, SparseCore 0:
  13.2 36.2 all-reduce.1
Sparse Core Ops, SparseCore 1:
  16.1 126.9 all-gather.1
where the time goes:
time: 168 us
  waiting for transfers between devices  124 us (74%)
  matrix products  16.9 us (10%)
  between operations  14.9 us (9%)
  local copies, waits for them, and re-layouts  10.4 us (6%)
  other arithmetic  1.89 us (1%)
    all_gather x1, waiting for transfers between devices, local(): lax.all_gather(own_lower, 'pcol', axis=0, tiled=True)  90.4 us
    psum x1, waiting for transfers between devices, local(): pivot_rows = lax.psum(picked, 'prow')  33.5 us
    dot_general x1, matrix products, local(): jnp.dot(lax.all_gather(own_lower, 'pcol', axis=0, tiled=True), upper_bloc...  11.2 us
    scatter x1, local copies, waits for them, and re-layouts, local(): return updated.at[target].set(upper_block, mode='drop')  6.39 us
    gather x1, local copies, waits for them, and re-layouts, local(): picked = jnp.where(inside[:, None], jnp.take(slab, safe_index, axis=0), 0.0)  3.76 us
  transfers between devices with their start and end apart: 2, of which 2 were waited for; matrix products, arithmetic and copies ran while one was open for 4% of the time, Pallas kernels for 0%

commit v1 on v0

--- a/solution.py
+++ b/solution.py
@@ -11,7 +11,7 @@
     inside = (local_index >= 0) & (local_index < row_count)
     safe_index = jnp.where(inside, local_index, 0)
     picked = jnp.where(inside[:, None], jnp.take(slab, safe_index, axis=0), 0.0)
-    pivot_rows = lax.psum(picked, "prow")
+    pivot_rows = lax.all_gather(picked, "prow").sum(axis=0)
     upper_block = jnp.dot(
         inv_lower, pivot_rows, precision=lax.Precision.HIGHEST, preferred_element_type=jnp.float32
     )

time: 168 us -> 189 us (1.12)
  waiting for transfers between devices: 124 us -> 145 us
    psum x1 -> x0, waiting for transfers between devices: 33.5 us -> none  [local(): pivot_rows = lax.psum(picked, 'prow')]
    all_gather x1, waiting for transfers between devices: 90.4 us -> 123 us  [local(): lax.all_gather(own_lower, 'pcol', axis=0, tiled=True)]
    all_gather x0 -> x1, waiting for transfers between devices: none -> 22.5 us  [local(): pivot_rows = lax.all_gather(picked, 'prow').sum(axis=0)]
where the time goes in v1:
time: 189 us
  waiting for transfers between devices  145 us (77%)
  matrix products  15.9 us (8%)
  between operations  13.5 us (7%)
  local copies, waits for them, and re-layouts  10.4 us (6%)
  other arithmetic  3.67 us (2%)
    all_gather x1, waiting for transfers between devices, local(): lax.all_gather(own_lower, 'pcol', axis=0, tiled=True)  123 us
    all_gather x1, waiting for transfers between devices, local(): pivot_rows = lax.all_gather(picked, 'prow').sum(axis=0)  22.5 us
    dot_general x1, matrix products, local(): jnp.dot(lax.all_gather(own_lower, 'pcol', axis=0, tiled=True), upper_bloc...  11.2 us
    scatter x1, local copies, waits for them, and re-layouts, local(): return updated.at[target].set(upper_block, mode='drop')  6.39 us
  transfers between devices with their start and end apart: 2, of which 2 were waited for; matrix products, arithmetic and copies ran while one was open for 4% of the time, Pallas kernels for 0%

profile of v1, /device:TPU:0, one launch (start us, length us, event | category | flops | bytes accessed | tf_op | source)
XLA Modules:
  0.0 188.7 jit_solution(8089885801633029652)
XLA Ops:
  6.5 0.0 copy-start
  6.5 0.0 copy-start.1
  6.5 0.0 all-gather.5.cloned.1.call-start
  6.5 0.8 compare_and_fusion
  7.4 0.0 copy-start.3
  7.4 3.8 %gather_fusion = f32[512,256]{1,0:T(8,128)S(1)} fusion(f32[4096,256]{1,0:T(8,128)} %param.5, s32[1024]{0:T(1024)S(1)} %pad_clamp_fusion), kind=kCustom, calls=%fused_computation | custom fusion | bytes 1050624 | tf_op jit(solution)/shard_map/jit(_take)/gather | solution.py:13
  11.2 1.0 fusion
  12.2 0.0 copy-start.2
  12.2 0.0 all-gather.5.cloned.1.call-update
  12.2 0.0 all-gather.3.cloned.1.call-start
  12.3 0.0 copy-done
  12.3 0.0 copy-done.1
  12.3 2.8 %fusion.1 = f32[512,512]{1,0:T(8,128)} fusion(f32[512,512]{1,0:T(8,128)S(1)} %copy-done, f32[512,512]{1,0:T(8,128)S(1)} %copy-done.1), kind=kOutput, calls=%fused_computation.10 | convolution fusion | flops 1610612736 | bytes 3145728 | tf_op jit(solution)/shard_map/dot_general | solution.py:18
  15.1 0.0 all-gather.3.cloned.1.call-update
  15.1 0.0 copy-done.3
  15.2 22.5 %all-gather.5.cloned.1.call-done = f32[4,512,256]{2,1,0:T(8,128)} async-done(((f32[1,512,256]{2,1,0:T(8,128)}), f32[4,512,256]{2,1,0:T(8,128)}) %all-gather.5.cloned.1.call-update) | async-done | bytes 2097168 | tf_op jit(solution)/shard_map/all_gather | solution.py:14
  37.7 1.8 reduce_sum.9
  39.5 0.0 copy-done.2
  39.5 1.9 fusion.2
  41.3 0.2 copy.7
  41.5 122.8 %all-gather.3.cloned.1.call-done = f32[4096,512]{1,0:T(8,128)} async-done(((f32[512,512]{1,0:T(8,128)}), f32[4096,512]{1,0:T(8,128)}) %all-gather.3.cloned.1.call-update) | async-done | bytes 8388624 | tf_op jit(solution)/shard_map/all_gather | solution.py:22
  164.3 11.2 %convolution_subtract_fusion = f32[4096,256]{1,0:T(8,128)} fusion(f32[4096,256]{1,0:T(8,128)} %param.5, f32[4096,512]{1,0:T(8,128)} %all-gather.3.cloned.1.call-done, f32[256,512]{1,0:T(8,128)S(1)} %fusion.2), kind=kOutput, calls=%fused_computation.2 | convolution fusion | flops 6443499520 | bytes 17301504 | tf_op jit(solution)/shard_map/dot_general | solution.py:21
  175.5 6.4 %scatter_fusion = f32[4096,256]{1,0:T(8,128)} fusion(f32[4096,256]{1,0:T(8,128)} %convolution_subtract_fusion, s32[512]{0:T(512)S(1)} %compare_select_fusion, f32[512,256]{1,0:T(8,128)S(1)} %copy.7), kind=kCustom, calls=%fused_computation.1 | custom fusion | bytes 1574912 | tf_op jit(solution)/shard_map/scatter | solution.py:29
  (2 shorter events, 0.0 us)
Async XLA Ops:
  6.5 5.7 %copy-start = (f32[512,512]{1,0:T(8,128)S(1)}, f32[512,512]{1,0:T(8,128)}, u32[]{:S(2)}) copy-start(f32[512,512]{1,0:T(8,128)} %param.6) | copy-start | bytes 3145732
  6.5 5.8 %copy-start.1 = (f32[512,512]{1,0:T(8,128)S(1)}, f32[512,512]{1,0:T(8,128)}, u32[]{:S(2)}) copy-start(f32[512,512]{1,0:T(8,128)} %param.9) | copy-start | bytes 3145732
  6.5 31.1 %all-gather.5.cloned.1.call-start = ((), (), s32[]{:S(2)}) async-start(), calls=%async_computation.1 | async-start | bytes 2621440 | tf_op jit(solution)/shard_map/all_gather | solution.py:14
  7.4 7.8 %copy-start.3 = (s32[512]{0:T(512)S(1)}, s32[512]{0:T(512)}, u32[]{:S(2)}) copy-start(s32[512]{0:T(512)} %param.7) | copy-start | bytes 6148
  12.2 27.3 %copy-start.2 = (f32[512,512]{1,0:T(8,128)S(1)}, f32[512,512]{1,0:T(8,128)}, u32[]{:S(2)}) copy-start(f32[512,512]{1,0:T(8,128)} %param.8) | copy-start | bytes 3145732
  12.2 152.1 %all-gather.3.cloned.1.call-start = ((), (), s32[]{:S(2)}) async-start(), calls=%async_computation | async-start | bytes 9437184 | tf_op jit(solution)/shard_map/all_gather | solution.py:22
Sparse Core Ops, SparseCore 0:
  12.4 25.2 all-gather.4
  39.8 124.4 all-gather.2

commit v2 on v0

--- a/solution.py
+++ b/solution.py
@@ -5,6 +5,13 @@
 
 
 def local(slab, panel, pivots, inv_lower, inv_upper):
+
+    def _supply_all_plane(matrix, which_dim, mesh_dim):
+        tall = lax.axis_size(mesh_dim)
+        arr_next = jnp.stack([matrix] * tall, axis=0)
+        f_next = lax.all_to_all(arr_next, axis_name=mesh_dim, split_axis=0, concat_axis=0)
+        return jnp.concatenate(f_next, axis=which_dim)
+
     row_count = slab.shape[0]
     first_row = lax.axis_index("prow") * row_count
     local_index = pivots - first_row
@@ -19,7 +26,7 @@
         panel, inv_upper, precision=lax.Precision.HIGHEST, preferred_element_type=jnp.float32
     )
     product = jnp.dot(
-        lax.all_gather(own_lower, "pcol", axis=0, tiled=True),
+        _supply_all_plane(own_lower, 0, "pcol"),
         upper_block,
         precision=lax.Precision.HIGHEST,
         preferred_element_type=jnp.float32,

time: 168 us -> 231 us (1.38)
  waiting for transfers between devices: 124 us -> 175 us
  starting transfers between devices: 0.05 us -> 7.48 us
  local copies, waits for them, and re-layouts: 10.4 us -> 16 us
    all_to_all x0 -> x1, waiting for transfers between devices: none -> 140 us  [_supply_all_plane(): lax.all_to_all(arr_next, axis_name=mesh_dim, split_axis=0, concat_axis=0)]
    all_gather x1 -> x0, waiting for transfers between devices: 90.4 us -> none  [local(): lax.all_gather(own_lower, 'pcol', axis=0, tiled=True)]
    all_to_all x0 -> x1, starting transfers between devices: none -> 7.44 us  [_supply_all_plane(): lax.all_to_all(arr_next, axis_name=mesh_dim, split_axis=0, concat_axis=0)]
    another operation x0 -> x1, local copies, waits for them, and re-layouts: none -> 4.3 us  [_supply_all_plane(): arr_next = jnp.stack([matrix] * tall, axis=0)]
  transfers between devices with their start and end apart: 2 -> 2, of which waited for: 2 -> 2; matrix products, arithmetic and copies ran while one was open for 4% -> 3% of each run, Pallas kernels for 0% -> 0%
where the time goes in v2:
time: 231 us; the launch traced here: 230 us
  waiting for transfers between devices  175 us (76%)
  matrix products  17.2 us (7%)
  local copies, waits for them, and re-layouts  16 us (7%)
  between operations  13.5 us (6%)
  starting transfers between devices  7.48 us (3%)
    all_to_all x1, waiting for transfers between devices, _supply_all_plane(): lax.all_to_all(arr_next, axis_name=mesh_dim, split_axis=0, concat_axis=0)  140 us
    psum x1, waiting for transfers between devices, local(): pivot_rows = lax.psum(picked, 'prow')  35 us
    dot_general x1, matrix products, local(): jnp.dot(_supply_all_plane(own_lower, 0, 'pcol'), upper_block, precision=l...  11.2 us
    all_to_all x1, starting transfers between devices, _supply_all_plane(): lax.all_to_all(arr_next, axis_name=mesh_dim, split_axis=0, concat_axis=0)  7.44 us
    scatter x1, local copies, waits for them, and re-layouts, local(): return updated.at[target].set(upper_block, mode='drop')  6.39 us
  transfers between devices with their start and end apart: 2, of which 2 were waited for; matrix products, arithmetic and copies ran while one was open for 3% of the time, Pallas kernels for 0%

profile of v2, /device:TPU:0, one launch (start us, length us, event | category | flops | bytes accessed | tf_op | source)
XLA Modules:
  0.0 230.2 jit_solution(7944536714986802093)
XLA Ops:
  6.5 0.0 copy-start
  6.5 1.2 copy-done
  7.8 3.1 %fusion = f32[512,512]{1,0:T(8,128)S(1)} fusion(f32[512,512]{1,0:T(8,128)S(1)} %copy-done, f32[512,512]{1,0:T(8,128)} %param.9), kind=kOutput, calls=%fused_computation.9 | convolution fusion | flops 1610612736 | bytes 3145728 | tf_op jit(solution)/shard_map/dot_general | solution.py:25
  10.8 4.3 %stack.2 = f32[8,512,512]{2,1,0:T(8,128)} broadcast(f32[512,512]{1,0:T(8,128)S(1)} %fusion), dimensions={1,2} | broadcast | bytes 9437184 | tf_op jit(solution)/shard_map/stack | solution.py:11
  15.1 0.0 copy-start.2
  15.1 7.4 %all-to-all-start = ((f32[8,512,512]{2,1,0:T(8,128)}), f32[8,512,512]{2,1,0:T(8,128)}, u32[]{:S(2)}, u32[]{:S(2)}) async-start(f32[8,512,512]{2,1,0:T(8,128)} %stack.2), calls=%async_computation | async-start | bytes 16777216 | tf_op jit(solution)/shard_map/all_to_all | solution.py:12
  22.6 0.0 copy-start.1
  22.6 0.0 all-reduce.2.cloned.1.call-start
  22.6 0.0 copy-done.2
  22.7 3.8 %gather_fusion = f32[512,256]{1,0:T(8,128)S(1)} fusion(f32[4096,256]{1,0:T(8,128)} %param.5, s32[1024]{0:T(1024)S(1)} %pad_clamp_fusion), kind=kCustom, calls=%fused_computation | custom fusion | bytes 1050624 | tf_op jit(solution)/shard_map/jit(_take)/gather | solution.py:20
  26.5 1.0 select_select_fusion
  27.5 0.0 all-reduce.2.cloned.1.call-update
  27.6 35.0 %all-reduce.2.cloned.1.call-done = f32[512,256]{1,0:T(8,128)} async-done(((f32[512,256]{1,0:T(8,128)}), f32[512,256]{1,0:T(8,128)}) %all-reduce.2.cloned.1.call-update) | async-done | bytes 524304 | tf_op jit(solution)/shard_map/psum | solution.py:21
  62.6 0.0 copy-done.1
  62.6 2.9 %fusion.1 = f32[256,512]{1,0:T(8,128)S(1)} fusion(f32[512,256]{1,0:T(8,128)} %all-reduce.2.cloned.1.call-done, f32[512,512]{1,0:T(8,128)S(1)} %copy-done.1), kind=kOutput, calls=%fused_computation.10 | convolution fusion | flops 805306368 | bytes 2097152 | tf_op jit(solution)/shard_map/dot_general | solution.py:22
  65.5 0.2 copy.6
  65.7 140.1 %all-to-all-done = f32[8,512,512]{2,1,0:T(8,128)} async-done(((f32[8,512,512]{2,1,0:T(8,128)}), f32[8,512,512]{2,1,0:T(8,128)}, u32[]{:S(2)}, u32[]{:S(2)}) %all-to-all-start) | async-done | bytes 8388640 | tf_op jit(solution)/shard_map/all_to_all | solution.py:12
  205.7 11.2 %convolution_subtract_fusion = f32[4096,256]{1,0:T(8,128)} fusion(f32[4096,256]{1,0:T(8,128)} %param.5, f32[4096,512]{1,0:T(8,128)} %bitcast, f32[256,512]{1,0:T(8,128)S(1)} %fusion.1), kind=kOutput, calls=%fused_computation.2 | convolution fusion | flops 6443499520 | bytes 17301504 | tf_op jit(solution)/shard_map/dot_general | solution.py:28
  216.9 6.4 %scatter_fusion = f32[4096,256]{1,0:T(8,128)} fusion(f32[4096,256]{1,0:T(8,128)} %convolution_subtract_fusion, s32[512]{0:T(512)S(1)} %compare_select_fusion, f32[512,256]{1,0:T(8,128)S(1)} %copy.6), kind=kCustom, calls=%fused_computation.1 | custom fusion | bytes 1574912 | tf_op jit(solution)/shard_map/scatter | solution.py:36
  (3 shorter events, 0.0 us)
Async XLA Ops:
  6.5 1.2 copy-start
  15.1 7.5 %copy-start.2 = (s32[512]{0:T(512)S(1)}, s32[512]{0:T(512)}, u32[]{:S(2)}) copy-start(s32[512]{0:T(512)} %param.7) | copy-start | bytes 6148
  15.1 190.6 %all-to-all-start = ((f32[8,512,512]{2,1,0:T(8,128)}), f32[8,512,512]{2,1,0:T(8,128)}, u32[]{:S(2)}, u32[]{:S(2)}) async-start(f32[8,512,512]{2,1,0:T(8,128)} %stack.2), calls=%async_computation | async-start | bytes 16777216 | tf_op jit(solution)/shard_map/all_to_all | solution.py:12
  22.6 40.0 %copy-start.1 = (f32[512,512]{1,0:T(8,128)S(1)}, f32[512,512]{1,0:T(8,128)}, u32[]{:S(2)}) copy-start(f32[512,512]{1,0:T(8,128)} %param.8) | copy-start | bytes 3145732
  22.6 40.0 %all-reduce.2.cloned.1.call-start = ((), (), s32[]{:S(2)}) async-start(), calls=%async_computation.1 | async-start | bytes 1048576 | tf_op jit(solution)/shard_map/psum | solution.py:21
Sparse Core Ops, SparseCore 0:
  27.7 34.8 all-reduce.1
